TPU v7x, 128 devices: a whole 4x4x4 slice. The times are simulated.
128 devices in a mesh: ctx: 16 (over x, z), head: 8 (over y, core).
Axes of the slice: x: 4, y: 4, z: 4, core: 2. Of those that a mesh axis runs over, the one named last changes fastest.
Arguments:
- input_x_channels: bfloat16 [16384, 8192], P('ctx', 'head'), may hold values from -4 to 4
- input_b_channels: bfloat16 [16384, 1024], P('ctx', 'head'), may hold values from -3 to 3
- input_c_channels: bfloat16 [16384, 1024], P('ctx', 'head'), may hold values from -3 to 3
- input_gate_channels: bfloat16 [16384, 8192], P('ctx', 'head'), may hold values from -75 to 75
- raw_step_sizes: float32 [128, 16384], P('head', 'ctx'), may hold values from -7 to 800
- log_decay_rate: float32 [128], P('head'), may hold values from -8 to -2.3
- head_skip_coeff: float32 [128], P('head'), may hold values from 0.5 to 2
- x_conv_taps: bfloat16 [4, 8192], P(None, 'head'), may hold values from -3 to 3
- b_conv_taps: bfloat16 [4, 1024], P(None, 'head'), may hold values from -3 to 3
- c_conv_taps: bfloat16 [4, 1024], P(None, 'head'), may hold values from -3 to 3
- gated_norm_gain: bfloat16 [8192], P('head'), may hold values from 0.099609375 to 1.8984375
- output_weight: bfloat16 [8192, 4096], P('head'), may hold values from -0.0625 to 0.0625
- adapter_down_panels: bfloat16 [96, 8192, 64], P('ctx', 'head'), may hold values from -0.0625 to 0.0625
- adapter_up_panels: bfloat16 [96, 64, 4096], P('ctx', None, 'head'), may hold values from -0.75 to 0.75
- turn_first_token: int32 [32], replicated, may hold values from 0 to 16256, as said below
- tenant_of_turn: int32 [32], replicated, may hold values from 0 to 95
- tenant_panel_index: int32 [96], replicated, may hold values from 0 to 95, each once
Outputs:
- out: bfloat16 [16384, 4096], P('ctx', 'head')
Inputs may be any that keep to these rules, and one draw needn't show every extreme that they name: `turn_first_token`: strictly increasing multiples of 128; the first is 0; every aligned block of 1024 tokens holds exactly 2 starts, and in every block but the first the earlier of them lies past the block's first token.
All inputs are finite; a program needn't handle non-finite values.
Results may differ from a plain program's by a relative error of at most 0.014.
Values may be sent and summed in bfloat16 or wider, within the bound.
A program may use at most 128 MiB of HBM per device.

v0:
```python
import jax
import jax.numpy as jnp
from jax import lax
from jax.sharding import PartitionSpec as P

P_SIZE = 64
N = 128
K = 4
Q = 128
TURN_DEV = 2
highest = lax.Precision.HIGHEST
epsilon = 1e-05


def shifted(block, axis, distance):
    devices = range(lax.axis_size(axis))
    route = [(i - distance, i) for i in devices if i - distance in devices]
    return lax.ppermute(block, axis, route)


def conv_rows(sequence, tail_rows, weight):
    token_rows = sequence.shape[0]
    joined = jnp.concatenate([tail_rows, sequence], axis=0).astype(jnp.float32)
    total = jnp.zeros((token_rows, sequence.shape[1]), jnp.float32)
    for tap in range(weight.shape[0]):
        total = total + weight[tap].astype(jnp.float32) * joined[tap : tap + token_rows]
    return jax.nn.silu(total).astype(jnp.bfloat16)


def local(
    input_x_channels,
    input_b_channels,
    input_c_channels,
    input_gate_channels,
    raw_step_sizes,
    log_decay_rate,
    head_skip_coeff,
    x_conv_taps,
    b_conv_taps,
    c_conv_taps,
    gated_norm_gain,
    output_weight,
    adapter_down_panels,
    adapter_up_panels,
    turn_first_token,
    tenant_of_turn,
    tenant_panel_index,
):
    token_rows = input_x_channels.shape[0]
    head_count = log_decay_rate.shape[0]
    group_count = input_b_channels.shape[1] // N
    per_group = head_count // group_count
    conv_edge = K - 1
    conv_tails = shifted(
        (
            input_x_channels[token_rows - conv_edge :],
            input_b_channels[token_rows - conv_edge :],
            input_c_channels[token_rows - conv_edge :],
        ),
        "ctx",
        1,
    )
    x_conv = conv_rows(input_x_channels, conv_tails[0], x_conv_taps)
    b_conv = conv_rows(input_b_channels, conv_tails[1], b_conv_taps)
    c_conv = conv_rows(input_c_channels, conv_tails[2], c_conv_taps)
    block_count = token_rows // Q
    step_sizes = jax.nn.softplus(raw_step_sizes)
    decay_rate = jnp.exp(log_decay_rate)
    step_heads = step_sizes.reshape(head_count, block_count, Q)
    running = jnp.cumsum(-step_heads * decay_rate[:, None, None], axis=2)
    run_blocks = running.transpose(1, 0, 2).reshape(block_count, group_count, per_group, Q)
    step_blocks = step_heads.transpose(1, 0, 2).reshape(block_count, group_count, per_group, Q)
    x_blocks = x_conv.astype(jnp.float32).reshape(block_count, Q, group_count, per_group, P_SIZE)
    b_blocks = b_conv.astype(jnp.float32).reshape(block_count, Q, group_count, N)
    c_blocks = c_conv.astype(jnp.float32).reshape(block_count, Q, group_count, N)
    scores = jnp.einsum("cqgn,ckgn->cgqk", c_blocks, b_blocks, precision=highest)
    causal = jnp.arange(Q)[:, None] >= jnp.arange(Q)[None, :]
    log_gap = run_blocks[..., :, None] - run_blocks[..., None, :]
    decay_mat = jnp.where(causal, jnp.exp(jnp.where(causal, log_gap, 0.0)), 0.0)
    mixing = scores[:, :, None] * decay_mat * step_blocks[..., None, :]
    y_local = jnp.einsum("cghqk,ckghp->cqghp", mixing, x_blocks, precision=highest)
    tail_weight = jnp.exp(run_blocks[..., -1:] - run_blocks) * step_blocks
    block_states = jnp.einsum(
        "cghk,ckghp,ckgn->cghpn", tail_weight, x_blocks, b_blocks, precision=highest
    )
    block_log = run_blocks[..., -1]

    def carry_step(carried, inputs):
        fresh_state, step_log = inputs
        return (jnp.exp(step_log)[..., None, None] * carried + fresh_state, carried)

    empty_state = jnp.zeros((group_count, per_group, P_SIZE, N), jnp.float32)
    device_state, before = lax.scan(carry_step, empty_state, (block_states, block_log))
    device_log = jnp.sum(block_log, axis=0)
    run_tokens = run_blocks.transpose(0, 3, 1, 2)
    y_local = y_local + jnp.exp(run_tokens)[..., None] * jnp.einsum(
        "cqgn,cghpn->cqghp", c_blocks, before, precision=highest
    )
    all_logs, states = (
        lax.all_gather(device_log[None], "ctx", axis=0, tiled=True),
        lax.all_gather(device_state[None], "ctx", axis=0, tiled=True),
    )
    device_count = all_logs.shape[0]
    own_index = lax.axis_index("ctx")
    order_index = jnp.arange(device_count)
    between = (order_index[:, None] < order_index[None, :]) & (order_index[None, :] < own_index)
    span_log = jnp.einsum("jk,kgh->jgh", between.astype(jnp.float32), all_logs, precision=highest)
    weights = jnp.where((order_index < own_index)[:, None, None], jnp.exp(span_log), 0.0)
    incoming = jnp.einsum("jgh,jghpn->ghpn", weights, states, precision=highest)
    start_log = jnp.cumsum(block_log, axis=0) - block_log
    device_running = start_log[:, None] + run_tokens
    y_value = y_local + jnp.exp(device_running)[..., None] * jnp.einsum(
        "cqgn,ghpn->cqghp", c_blocks, incoming, precision=highest
    )
    y_value = y_value + head_skip_coeff.reshape(group_count, per_group)[:, :, None] * x_blocks
    group_width = per_group * P_SIZE
    gated = y_value.reshape(token_rows, group_count, group_width) * jax.nn.silu(
        input_gate_channels.astype(jnp.float32)
    ).reshape(token_rows, group_count, group_width)
    norm_scale = lax.rsqrt(jnp.mean(gated * gated, axis=2, keepdims=True) + epsilon)
    y_normed = (
        (gated * norm_scale).reshape(token_rows, -1) * gated_norm_gain.astype(jnp.float32)
    ).astype(jnp.bfloat16)
    own_index = lax.axis_index("ctx")
    slot_count = TURN_DEV + 1
    slot_turns = TURN_DEV * own_index - 1 + jnp.arange(slot_count)
    clipped = jnp.maximum(slot_turns, 0)
    tenants = jnp.take(tenant_of_turn, clipped)
    slot_homes = jnp.take(tenant_panel_index, tenants)
    all_down, all_up = (
        lax.all_gather(adapter_down_panels, "ctx", axis=0, tiled=True),
        lax.all_gather(adapter_up_panels, "ctx", axis=0, tiled=True),
    )
    down_slots = jnp.take(all_down, slot_homes, axis=0)
    up_slots = jnp.take(all_up, slot_homes, axis=0)
    base_out = lax.psum_scatter(
        jnp.dot(y_normed, output_weight, preferred_element_type=jnp.float32).astype(jnp.bfloat16),
        "head",
        scatter_dimension=1,
        tiled=True,
    ).astype(jnp.float32)
    own_starts = lax.dynamic_slice_in_dim(turn_first_token, TURN_DEV * own_index, TURN_DEV, 0)
    token_place = own_index * token_rows + jnp.arange(token_rows)
    token_slot = jnp.sum((token_place[:, None] >= own_starts[None, :]).astype(jnp.int32), axis=1)
    slot_mask = (token_slot[:, None] == jnp.arange(slot_count)[None, :]).astype(jnp.float32)
    low_slots = jnp.einsum("tc,scr->tsr", y_normed, down_slots, preferred_element_type=jnp.float32)
    rank_reduced = jnp.sum(low_slots * slot_mask[:, :, None], axis=1)
    rank_reduced = lax.psum(rank_reduced, "head").astype(jnp.bfloat16)
    adapter_out = jnp.einsum(
        "tr,srd->tsd", rank_reduced, up_slots, preferred_element_type=jnp.float32
    )
    adapter_out = jnp.sum(adapter_out * slot_mask[:, :, None], axis=1)
    return (base_out + adapter_out).astype(jnp.bfloat16)


def solution(mesh):
    in_specs = (
        P("ctx", "head"),
        P("ctx", "head"),
        P("ctx", "head"),
        P("ctx", "head"),
        P("head", "ctx"),
        P("head"),
        P("head"),
        P(None, "head"),
        P(None, "head"),
        P(None, "head"),
        P("head"),
        P("head", None),
        P("ctx", "head", None),
        P("ctx", None, "head"),
        P(),
        P(),
        P(),
    )
    out_specs = P("ctx", "head")
    return jax.shard_map(local, mesh=mesh, in_specs=in_specs, out_specs=out_specs, check_vma=False)
```

profile of v0, /device:TPU:0, one launch (start us, length us, event | category | flops | bytes accessed | tf_op | source)
XLA Modules:
  0.0 349.8 jit_solution(5705735439827553091)
XLA Ops:
  8.2 3.9 %collective-permute-start = (bf16[3,1024]{0,1:T(8,128)(2,1)}, bf16[3,1024]{0,1:T(8,128)(2,1)S(1)}, u32[]{:S(2)}, u32[]{:S(2)}) collective-permute-start(bf16[3,1024]{0,1:T(8,128)(2,1)} %copy.74), channel_id=1, source_target_pairs={{0,8},{8,16},{16,24},{24,32},{32,40},{40,48},{48,56},{56,64},{64,7... | collective-permute-start | bytes 18440 | tf_op jit(solution)/shard_map/ppermute | solution.py:18
  12.8 3.8 %collective-permute-start.2 = (bf16[3,128]{1,0:T(4,128)(2,1)S(1)}, bf16[3,128]{1,0:T(4,128)(2,1)S(1)}, u32[]{:S(2)}, u32[]{:S(2)}) collective-permute-start(bf16[3,128]{1,0:T(4,128)(2,1)S(1)} %slice.104), channel_id=1, source_target_pairs={{0,8},{8,16},{16,24},{24,32},{32,40},{40,48},{48,56},{56,64},{64,7... | collective-permute-start | bytes 2312 | tf_op jit(solution)/shard_map/ppermute | solution.py:18
  19.1 4.5 %reduce_window_sum.22 = f32[16,8,128]{2,1,0:T(8,128)S(1)} reduce-window(f32[16,8,128]{2,1,0:T(8,128)S(1)} %negate_multiply_fusion, f32[]{:T(128)} %constant.95.clone.1), window={size=1x1x128 pad=0_0x0_0x127_0}, to_apply=%region_0.1 | reduce-window | flops 2080768 | bytes 131076 | tf_op jit(solution)/shard_map/jit(cumsum)/reduce_window_sum | solution.py:70
  25.0 2.9 copy.75
  28.5 1.2 maximum_convert_fusion
  29.7 5.5 %convert_bitcast_fusion = (f32[128,8,8,128]{3,1,2,0:T(8,128)}, bf16[1024,1024]{0,1:T(8,128)(2,1)S(1)}) fusion(f32[1027,1024]{0,1:T(8,128)S(1)} %maximum_convert_fusion, f32[1024]{0:T(1024)S(1)} %bitcast.186, f32[1024]{0:T(1024)S(1)} %bitcast.187, f32[1024]{0:T(1024)S(1)} %bitcast.185, f32[1024]{0:T(1024)S(1)} %bitcast.184), kind=kLoop, calls=%fused_computation.43 | loop fusion | flops 13631488 | bytes 23085056
  36.2 3.8 %fusion.31 = f32[8,1,16,64,128]{4,3,2,1,0:T(8,128)} fusion(bf16[8,128,128,1]{2,1,3,0:T(8,128)(2,1)S(1)} %bitcast.173, f32[8,128,16,64]{1,0,3,2:T(8,128)S(1)} %convert_multiply_fusion.1), kind=kOutput, calls=%fused_computation.55 | convolution fusion | flops 1610612736 | bytes 8650752 | tf_op jit(solution)/shard_map/cghk,ckghp,ckgn->cghpn/dot_general | solution.py:83
  40.0 16.3 %while.13 = (s32[]{:T(128)}, f32[1,16,64,128]{3,2,1,0:T(8,128)S(1)}, f32[8,1,16,64,128]{4,3,2,1,0:T(8,128)}, f32[8,1,16]{2,1,0:T(1,128)S(1)}, f32[8,1,16,64,128]{4,3,2,1,0:T(8,128)}, /*index=5*/s32[]{:T(128)}, s32[]{:T(128)}) while((s32[]{:T(128)}, f32[1,16,64,128]{3,2,1,0:T(8,128)S(1)}, f32[8,1,16,64,128]{4,3,2,1,0:T(8,128)}, ...), condition=%wide.region_2.3_spmd.clone, body=%wide.region_1.2_spmd.clone.sunk | while | flops 524291 | bytes 2622240 | solution.py:93
  40.9 1.2 bitcast_add_fusion.2
  51.1 1.2 bitcast_add_fusion.2
  58.7 3.5 %collective-permute-start.1 = (bf16[3,128]{1,0:T(4,128)(2,1)S(1)}, bf16[3,128]{1,0:T(4,128)(2,1)S(1)}, u32[]{:S(2)}, u32[]{:S(2)}) collective-permute-start(bf16[3,128]{1,0:T(4,128)(2,1)S(1)} %slice.95), channel_id=1, source_target_pairs={{0,8},{8,16},{16,24},{24,32},{32,40},{40,48},{48,56},{56,64},{64,7... | collective-permute-start | bytes 2312 | tf_op jit(solution)/shard_map/ppermute | solution.py:18
  63.9 36.2 %all-reduce = f32[256]{0:T(256)S(1)} all-reduce(f32[256]{0:T(256)S(1)} %dynamic-update-slice), channel_id=2, replica_groups=mesh['ctx'=16,'head'=8] {'ctx'}, use_global_device_ids=true, to_apply=%add | all-reduce | flops 256 | bytes 2048
  100.7 4.0 %copy.92 = bf16[1024,1024]{0,1:T(8,128)(2,1)} copy(bf16[1024,1024]{1,0:T(8,128)(2,1)} %param.22) | data formatting | bytes 4194304 | tf_op args[3]
  105.4 1.5 copy-done.3
  106.9 3.0 copy.104
  110.1 3.5 %fusion.21 = f32[8,16,64,128]{3,2,1,0:T(8,128)} fusion(bf16[8,128,128,1]{2,1,3,0:T(8,128)(2,1)S(1)} %bitcast.170, f32[8,1,16,64,128]{4,3,2,1,0:T(8,128)S(1)} %copy-done.8), kind=kOutput, calls=%fused_computation.38 | convolution fusion | flops 1610612736 | bytes 8650752 | tf_op jit(solution)/shard_map/cqgn,cghpn->cqghp/dot_general | solution.py:96
  113.6 11.3 %fusion.4 = f32[8,16,64,128]{3,2,1,0:T(8,128)} fusion(f32[8,16,128]{2,1,0:T(8,128)S(1)} %copy.78, f32[8,16,128]{2,1,0:T(8,128)S(1)} %copy.76, f32[8,128,128]{2,1,0:T(8,128)S(1)} %fusion.61, pred[128,128]{1,0:T(8,128)(4,1)S(1)} %iota_compare_fusion, bf16[8,128,16,64]{1,0,3,2:T(8,128)(2,1)S(1)} %bitcast.167), kind=kOutput, calls=%fused_computation.11 | convolution fusion | flops 1621098496 | bytes 6963200 | tf_op jit(solution)/shard_map/cghqk,ckghp->cqghp/dot_general | solution.py:81
  124.9 3.8 %all-gather.10.cloned.1.call-done = f32[16,16,64,128]{3,2,1,0:T(8,128)} async-done(((f32[1,16,64,128]{3,2,1,0:T(8,128)}), f32[16,16,64,128]{3,2,1,0:T(8,128)}) %all-gather.10.cloned.1.call-update) | async-done | bytes 8388624 | tf_op jit(solution)/shard_map/all_gather | solution.py:101
  128.7 12.8 %fusion.2 = f32[16,1,64,128]{3,1,2,0:T(1,128)S(1)} fusion(f32[16,16,1,1]{0,2,3,1:T(1,128)S(1)} %copy.96, f32[16,16,64,128]{3,2,1,0:T(8,128)} %all-gather.10.cloned.1.call-done), kind=kOutput, calls=%fused_computation.9 | convolution fusion | flops 25165824 | bytes 8913920 | tf_op jit(solution)/shard_map/jgh,jghpn->ghpn/dot_general | solution.py:109
  141.5 5.1 %fusion.19 = f32[8,128,1,16,64]{1,4,3,0,2:T(8,128)S(1)} fusion(f32[8,16,64,128]{3,2,1,0:T(8,128)S(1)} %copy-done.6, f32[8,16,64,128]{3,2,1,0:T(8,128)} %fusion.4, f32[8,128,1,16,64]{1,0,4,3,2:T(8,128)S(1)} %bitcast.164, f32[16,64,128,1]{2,1,0,3:T(8,128)S(1)} %bitcast.175, bf16[8,128,128,1]{2,1,3,0:T(8,128)(2,1)S(1)} %bitcast.171, f32[16]{0:T(128)S(1)} %copy-done.13, ...), kind=kOutput, calls=%fused_computation.35 | convolution fusion | flops 1616904192 | bytes 17694784 | tf_op jit(solution)/shard_map/cqgn,ghpn->cqghp/dot_general | solution.py:112
  146.6 3.3 copy.91
  150.0 1.7 multiply_reduce_fusion.1
  151.8 2.0 copy-done.4
  153.8 11.5 %convolution_convert_fusion = bf16[1024,4096]{1,0:T(8,128)(2,1)} fusion(bf16[1024,4096]{1,0:T(8,128)(2,1)S(1)} %bitcast.189, f32[1024,1024]{0,1:T(8,128)S(1)} %get-tuple-element.84, f32[1024]{0:T(1024)S(1)} %convert_element_type.84, f32[1024]{0:T(1024)S(1)} %add_rsqrt_fusion), kind=kOutput, calls=%fused_computation.18 | convolution fusion | flops 8597274624 | bytes 20979712 | tf_op jit(solution)/shard_map/dot_general | solution.py:137
  166.9 24.9 %all-gather.8.cloned.1.call-done = bf16[96,64,512]{2,1,0:T(8,128)(2,1)} async-done(((bf16[6,64,512]{2,1,0:T(8,128)(2,1)}), bf16[96,64,512]{2,1,0:T(8,128)(2,1)}) %all-gather.8.cloned.1.call-update) | async-done | bytes 6291472 | tf_op jit(solution)/shard_map/all_gather | solution.py:132
  191.8 3.3 gather_fusion.3
  195.1 88.6 %all-gather.6.cloned.1.call-done = bf16[96,1024,64]{1,2,0:T(8,128)(2,1)} async-done(((bf16[6,1024,64]{1,2,0:T(8,128)(2,1)}), bf16[96,1024,64]{1,2,0:T(8,128)(2,1)}) %all-gather.6.cloned.1.call-update) | async-done | bytes 12582928 | tf_op jit(solution)/shard_map/all_gather | solution.py:131
  283.7 5.1 %gather_fusion.2 = bf16[3,1024,64]{1,2,0:T(8,128)(2,1)S(1)} fusion(bf16[96,1024,64]{1,2,0:T(8,128)(2,1)} %all-gather.6.cloned.1.call-done, s32[1024]{0:T(1024)S(1)} %pad_clamp_fusion), kind=kCustom, calls=%fused_computation.2 | custom fusion | bytes 786444 | tf_op jit(solution)/shard_map/jit(_take)/gather | solution.py:134
  289.0 2.9 fusion.59
  291.9 31.3 %all-reduce.2 = bf16[1024,64]{0,1:T(8,128)(2,1)S(1)} all-reduce(f32[1024,64]{0,1:T(8,128)S(1)} %multiply_reduce_fusion.2), channel_id=1, replica_groups=mesh['ctx'=16,'head'=8] {'head'}, use_global_device_ids=true, to_apply=%region_9.10 | all-reduce | flops 65536 | bytes 393216 | tf_op jit(solution)/shard_map/psum | solution.py:148
  324.3 16.4 %reduce-scatter.2.cloned.1.call-done = bf16[1024,512]{1,0:T(8,128)(2,1)} async-done(((bf16[1024,4096]{1,0:T(8,128)(2,1)}), bf16[1024,512]{1,0:T(8,128)(2,1)}) %reduce-scatter.2.cloned.1.call-update) | async-done | bytes 1048592 | tf_op jit(solution)/shard_map/reduce_scatter | solution.py:136
  340.7 2.6 add_convert_fusion
  (126 shorter events, 29.0 us)
Async XLA Ops:
  6.5 158.8 %copy-start = (s32[32]{0:T(128)S(1)}, s32[32]{0:T(128)}, u32[]{:S(2)}) copy-start(s32[32]{0:T(128)} %param.34) | copy-start | bytes 388
  6.5 21.5 %copy-start.9 = (bf16[1024,128]{1,0:T(8,128)(2,1)S(1)}, bf16[1024,128]{1,0:T(8,128)(2,1)}, u32[]{:S(2)}) copy-start(bf16[1024,128]{1,0:T(8,128)(2,1)} %param.20) | copy-start | bytes 786436
  6.5 122.1 %all-gather.10.cloned.1.call-start = ((), (), s32[]{:S(2)}) async-start(), calls=%async_computation.4 | async-start | bytes 8912896 | tf_op jit(solution)/shard_map/all_gather | solution.py:101
  8.2 20.3 %collective-permute-start = (bf16[3,1024]{0,1:T(8,128)(2,1)}, bf16[3,1024]{0,1:T(8,128)(2,1)S(1)}, u32[]{:S(2)}, u32[]{:S(2)}) collective-permute-start(bf16[3,1024]{0,1:T(8,128)(2,1)} %copy.74), channel_id=1, source_target_pairs={{0,8},{8,16},{16,24},{24,32},{32,40},{40,48},{48,56},{56,64},{64,7... | collective-permute-start | bytes 18440 | tf_op jit(solution)/shard_map/ppermute | solution.py:18
  12.8 15.2 %collective-permute-start.2 = (bf16[3,128]{1,0:T(4,128)(2,1)S(1)}, bf16[3,128]{1,0:T(4,128)(2,1)S(1)}, u32[]{:S(2)}, u32[]{:S(2)}) collective-permute-start(bf16[3,128]{1,0:T(4,128)(2,1)S(1)} %slice.104), channel_id=1, source_target_pairs={{0,8},{8,16},{16,24},{24,32},{32,40},{40,48},{48,56},{56,64},{64,7... | collective-permute-start | bytes 2312 | tf_op jit(solution)/shard_map/ppermute | solution.py:18
  40.0 18.7 %copy-start.10 = (bf16[1024,128]{1,0:T(8,128)(2,1)S(1)}, bf16[1024,128]{1,0:T(8,128)(2,1)}, u32[]{:S(2)}) copy-start(bf16[1024,128]{1,0:T(8,128)(2,1)} %param.21) | copy-start | bytes 786436
  40.0 22.2 %copy-start.15 = (u32[128]{0:T(128)S(1)}, u32[128]{0:T(128)}, u32[]{:S(2)}) copy-start(u32[128]{0:T(128)} %constant.114) | copy-start | bytes 1540
  40.0 60.3 %copy-start.11 = (bf16[4,128]{1,0:T(4,128)(2,1)S(1)}, bf16[4,128]{1,0:T(4,128)(2,1)}, u32[]{:S(2)}) copy-start(bf16[4,128]{1,0:T(4,128)(2,1)} %param.28) | copy-start | bytes 3076
  56.3 0.8 copy-start.2
  56.3 48.3 %copy-start.12 = (bf16[1024]{0:T(1024)(128)(2,1)S(1)}, bf16[1024]{0:T(1024)(128)(2,1)}, u32[]{:S(2)}) copy-start(bf16[1024]{0:T(1024)(128)(2,1)} %param.29) | copy-start | bytes 6148
  57.1 134.6 %all-gather.8.cloned.1.call-start = ((), (), s32[]{:S(2)}) async-start(), calls=%async_computation.3 | async-start | bytes 6684672 | tf_op jit(solution)/shard_map/all_gather | solution.py:132
  57.9 225.8 %all-gather.6.cloned.1.call-start = ((), (), s32[]{:S(2)}) async-start(), calls=%async_computation.2 | async-start | bytes 13369344 | tf_op jit(solution)/shard_map/all_gather | solution.py:131
  58.6 282.1 %reduce-scatter.2.cloned.1.call-start = ((), (), s32[]{:S(2)}) async-start(), calls=%async_computation.1 | async-start | bytes 9437184 | tf_op jit(solution)/shard_map/reduce_scatter | solution.py:136
  58.7 46.0 %collective-permute-start.1 = (bf16[3,128]{1,0:T(4,128)(2,1)S(1)}, bf16[3,128]{1,0:T(4,128)(2,1)S(1)}, u32[]{:S(2)}, u32[]{:S(2)}) collective-permute-start(bf16[3,128]{1,0:T(4,128)(2,1)S(1)} %slice.95), channel_id=1, source_target_pairs={{0,8},{8,16},{16,24},{24,32},{32,40},{40,48},{48,56},{56,64},{64,7... | collective-permute-start | bytes 2312 | tf_op jit(solution)/shard_map/ppermute | solution.py:18
  104.6 2.2 copy-start.3
  106.9 3.2 copy-start.8
  124.9 16.7 %copy-start.13 = (f32[16]{0:T(128)S(1)}, f32[16]{0:T(128)}, u32[]{:S(2)}) copy-start(f32[16]{0:T(128)} %param.25) | copy-start | bytes 196
  128.7 12.9 %copy-start.5 = (f32[128,8,8,128]{3,2,1,0:T(8,128)S(1)}, f32[128,8,8,128]{3,2,1,0:T(8,128)}, u32[]{:S(2)}) copy-start(f32[128,8,8,128]{3,2,1,0:T(8,128)} %copy.104) | copy-start | bytes 12582916
  128.7 12.9 %copy-start.6 = (f32[8,16,64,128]{3,2,1,0:T(8,128)S(1)}, f32[8,16,64,128]{3,2,1,0:T(8,128)}, u32[]{:S(2)}) copy-start(f32[8,16,64,128]{3,2,1,0:T(8,128)} %fusion.21) | copy-start | bytes 12582916
  146.6 3.3 copy-start.7
  146.6 7.2 %slice-start = ((s8[8388608]{0:T(1024)(128)(4,1)}), s8[4194304]{0:T(1024)(128)(4,1)S(1)}, s32[]{:S(2)}) async-start(s8[8388608]{0:T(1024)(128)(4,1)} %bitcast.188), calls=%async_computation.5 | async-start | bytes 8388608
  150.0 3.8 %slice-start.1 = ((s8[8388608]{0:T(1024)(128)(4,1)}), s8[4194304]{0:T(1024)(128)(4,1)S(1)}, s32[]{:S(2)}) async-start(s8[8388608]{0:T(1024)(128)(4,1)} %bitcast.188), calls=%async_computation.6 | async-start | bytes 8388608
  151.7 2.0 copy-start.4
  165.3 0.7 copy-start.1
  165.3 1.4 copy-start.14
Sparse Core Ops, SparseCore 0:
  57.3 71.3 all-gather.9
  130.8 60.8 all-gather.7
  194.0 89.7 all-gather.5
  286.0 54.6 reduce-scatter.1
where the time goes:
time: 351 us; the launch traced here: 350 us
  waiting for transfers between devices  135 us (38%)
  blocking collectives  67.5 us (19%)
  matrix products  52.3 us (15%)
  other arithmetic  36.4 us (10%)
  local copies, waits for them, and re-layouts  32.7 us (9%)
  between operations  14.3 us (4%)
  starting transfers between devices  11.4 us (3%)
    all_gather x1, waiting for transfers between devices, local(): lax.all_gather(adapter_down_panels, 'ctx', axis=0, tiled=True)  88.6 us
    unnamed x1, blocking collectives  36.2 us
    psum x1, blocking collectives, local(): rank_reduced = lax.psum(rank_reduced, 'head').astype(jnp.bfloat16)  31.3 us
    all_gather x1, waiting for transfers between devices, local(): lax.all_gather(adapter_up_panels, 'ctx', axis=0, tiled=True)  24.9 us
    reduce_scatter x1, waiting for transfers between devices, local(): lax.psum_scatter(jnp.dot(y_normed, output_weight, preferred_element_type=...  16.4 us
    unnamed x44, local copies, waits for them, and re-layouts  15.9 us
    dot_general x1, matrix products, local(): incoming = jnp.einsum('jgh,jghpn->ghpn', weights, states, precision=highest)  12.8 us
    dot_general x1, matrix products, local(): jnp.dot(y_normed, output_weight, preferred_element_type=jnp.float32)  11.5 us
  transfers between devices with their start and end apart: 7, of which 4 were waited for; matrix products, arithmetic and copies ran while one was open for 24% of the time, Pallas kernels for 0%

commit v1 on v0

--- a/solution.py
+++ b/solution.py
@@ -2,6 +2,7 @@
 import jax.numpy as jnp
 from jax import lax
 from jax.sharding import PartitionSpec as P
+from jax.lax import all_gather
 
 P_SIZE = 64
 N = 128
@@ -145,7 +146,8 @@
     slot_mask = (token_slot[:, None] == jnp.arange(slot_count)[None, :]).astype(jnp.float32)
     low_slots = jnp.einsum("tc,scr->tsr", y_normed, down_slots, preferred_element_type=jnp.float32)
     rank_reduced = jnp.sum(low_slots * slot_mask[:, :, None], axis=1)
-    rank_reduced = lax.psum(rank_reduced, "head").astype(jnp.bfloat16)
+    _view_lines = lambda content: jnp.sum(all_gather(content, "head"), axis=0)
+    rank_reduced = _view_lines(rank_reduced).astype(jnp.bfloat16)
     adapter_out = jnp.einsum(
         "tr,srd->tsd", rank_reduced, up_slots, preferred_element_type=jnp.float32
     )

time: 351 us -> 376 us (1.071)
  waiting for transfers between devices: 135 us -> 182 us
  blocking collectives: 67.5 us -> 36.2 us
  matrix products: 52.3 us -> 56.6 us
    reduce_scatter x1, waiting for transfers between devices: 16.4 us -> 50.5 us  [local(): lax.psum_scatter(jnp.dot(y_normed, output_weight, preferred_element_type=...]
    psum x1 -> x0, blocking collectives: 31.3 us -> none  [local(): rank_reduced = lax.psum(rank_reduced, 'head').astype(jnp.bfloat16)]
    all_gather x0 -> x1, waiting for transfers between devices: none -> 23 us  [local(): _view_lines = lambda content: jnp.sum(all_gather(content, 'head'), axis=0)]
    all_gather x1, waiting for transfers between devices: 88.6 us -> 66.4 us  [local(): lax.all_gather(adapter_down_panels, 'ctx', axis=0, tiled=True)]
    all_gather x1, waiting for transfers between devices: 24.9 us -> 38.6 us  [local(): lax.all_gather(adapter_up_panels, 'ctx', axis=0, tiled=True)]
    dot_general x1, matrix products: 11.5 us -> 15.6 us  [local(): jnp.dot(y_normed, output_weight, preferred_element_type=jnp.float32)]
    unnamed x44 -> x41, local copies, waits for them, and re-layouts: 15.9 us -> 16.7 us
  transfers between devices with their start and end apart: 7 -> 8, of which waited for: 4 -> 5; matrix products, arithmetic and copies ran while one was open for 24% -> 26% of each run, Pallas kernels for 0% -> 0%
where the time goes in v1:
time: 376 us; the launch traced here: 374 us
  waiting for transfers between devices  182 us (48%)
  matrix products  56.6 us (15%)
  other arithmetic  40.1 us (11%)
  blocking collectives  36.2 us (10%)
  local copies, waits for them, and re-layouts  33.5 us (9%)
  between operations  14.2 us (4%)
  starting transfers between devices  11.4 us (3%)
    all_gather x1, waiting for transfers between devices, local(): lax.all_gather(adapter_down_panels, 'ctx', axis=0, tiled=True)  66.4 us
    reduce_scatter x1, waiting for transfers between devices, local(): lax.psum_scatter(jnp.dot(y_normed, output_weight, preferred_element_type=...  50.5 us
    all_gather x1, waiting for transfers between devices, local(): lax.all_gather(adapter_up_panels, 'ctx', axis=0, tiled=True)  38.6 us
    unnamed x1, blocking collectives  36.2 us
    all_gather x1, waiting for transfers between devices, local(): _view_lines = lambda content: jnp.sum(all_gather(content, 'head'), axis=0)  23 us
    unnamed x41, local copies, waits for them, and re-layouts  16.7 us
    dot_general x1, matrix products, local(): jnp.dot(y_normed, output_weight, preferred_element_type=jnp.float32)  15.6 us
    dot_general x1, matrix products, local(): incoming = jnp.einsum('jgh,jghpn->ghpn', weights, states, precision=highest)  12.8 us
  transfers between devices with their start and end apart: 8, of which 5 were waited for; matrix products, arithmetic and copies ran while one was open for 26% of the time, Pallas kernels for 0%

profile of v1, /device:TPU:0, one launch (start us, length us, event | category | flops | bytes accessed | tf_op | source)
XLA Modules:
  0.0 374.3 jit_solution(16101727310976549852)
XLA Ops:
  8.2 3.9 %collective-permute-start = (bf16[3,1024]{0,1:T(8,128)(2,1)}, bf16[3,1024]{0,1:T(8,128)(2,1)S(1)}, u32[]{:S(2)}, u32[]{:S(2)}) collective-permute-start(bf16[3,1024]{0,1:T(8,128)(2,1)} %copy.73), channel_id=1, source_target_pairs={{0,8},{8,16},{16,24},{24,32},{32,40},{40,48},{48,56},{56,64},{64,7... | collective-permute-start | bytes 18440 | tf_op jit(solution)/shard_map/ppermute | solution.py:19
  12.8 3.8 %collective-permute-start.2 = (bf16[3,128]{1,0:T(4,128)(2,1)S(1)}, bf16[3,128]{1,0:T(4,128)(2,1)S(1)}, u32[]{:S(2)}, u32[]{:S(2)}) collective-permute-start(bf16[3,128]{1,0:T(4,128)(2,1)S(1)} %slice.104), channel_id=1, source_target_pairs={{0,8},{8,16},{16,24},{24,32},{32,40},{40,48},{48,56},{56,64},{64,7... | collective-permute-start | bytes 2312 | tf_op jit(solution)/shard_map/ppermute | solution.py:19
  19.1 4.5 %reduce_window_sum.22 = f32[16,8,128]{2,1,0:T(8,128)S(1)} reduce-window(f32[16,8,128]{2,1,0:T(8,128)S(1)} %negate_multiply_fusion, f32[]{:T(128)} %constant.95.clone.1), window={size=1x1x128 pad=0_0x0_0x127_0}, to_apply=%region_0.1 | reduce-window | flops 2080768 | bytes 131076 | tf_op jit(solution)/shard_map/jit(cumsum)/reduce_window_sum | solution.py:71
  25.0 2.9 copy.74
  28.5 1.2 maximum_convert_fusion
  29.7 5.4 %convert_bitcast_fusion = (f32[128,8,8,128]{3,1,2,0:T(8,128)}, bf16[1024,1024]{0,1:T(8,128)(2,1)S(1)}) fusion(f32[1027,1024]{0,1:T(8,128)S(1)} %maximum_convert_fusion, f32[1024]{0:T(1024)S(1)} %bitcast.192, f32[1024]{0:T(1024)S(1)} %bitcast.193, f32[1024]{0:T(1024)S(1)} %bitcast.191, f32[1024]{0:T(1024)S(1)} %bitcast.190), kind=kLoop, calls=%fused_computation.43 | loop fusion | flops 13631488 | bytes 23085056
  36.2 3.8 %fusion.31 = f32[8,1,16,64,128]{4,3,2,1,0:T(8,128)} fusion(bf16[8,128,128,1]{2,1,3,0:T(8,128)(2,1)S(1)} %bitcast.178, f32[8,128,16,64]{1,0,3,2:T(8,128)S(1)} %convert_multiply_fusion.1), kind=kOutput, calls=%fused_computation.55 | convolution fusion | flops 1610612736 | bytes 8650752 | tf_op jit(solution)/shard_map/cghk,ckghp,ckgn->cghpn/dot_general | solution.py:84
  40.0 16.3 %while.13 = (s32[]{:T(128)}, f32[1,16,64,128]{3,2,1,0:T(8,128)S(1)}, f32[8,1,16,64,128]{4,3,2,1,0:T(8,128)}, f32[8,1,16]{2,1,0:T(1,128)S(1)}, f32[8,1,16,64,128]{4,3,2,1,0:T(8,128)}, /*index=5*/s32[]{:T(128)}, s32[]{:T(128)}) while((s32[]{:T(128)}, f32[1,16,64,128]{3,2,1,0:T(8,128)S(1)}, f32[8,1,16,64,128]{4,3,2,1,0:T(8,128)}, ...), condition=%wide.region_2.3_spmd.clone, body=%wide.region_1.2_spmd.clone.sunk | while | flops 524291 | bytes 2622240 | solution.py:94
  42.9 1.2 bitcast_add_fusion.2
  45.0 1.2 bitcast_add_fusion.2
  58.8 3.5 collective-permute-start.1
  63.9 36.2 %all-reduce = f32[256]{0:T(256)S(1)} all-reduce(f32[256]{0:T(256)S(1)} %dynamic-update-slice), channel_id=2, replica_groups=mesh['ctx'=16,'head'=8] {'ctx'}, use_global_device_ids=true, to_apply=%add | all-reduce | flops 256 | bytes 2048
  102.3 4.0 %copy.91 = bf16[1024,1024]{0,1:T(8,128)(2,1)} copy(bf16[1024,1024]{1,0:T(8,128)(2,1)} %param.22) | data formatting | bytes 4194304 | tf_op args[3]
  107.0 1.6 copy-done.4
  108.6 3.1 copy.103
  111.7 3.5 fusion.21
  115.2 11.3 %fusion.4 = f32[8,16,64,128]{3,2,1,0:T(8,128)} fusion(f32[8,16,128]{2,1,0:T(8,128)S(1)} %copy.77, f32[8,16,128]{2,1,0:T(8,128)S(1)} %copy.75, f32[8,128,128]{2,1,0:T(8,128)S(1)} %fusion.61, pred[128,128]{1,0:T(8,128)(4,1)S(1)} %iota_compare_fusion, bf16[8,128,16,64]{1,0,3,2:T(8,128)(2,1)S(1)} %bitcast.172), kind=kOutput, calls=%fused_computation.11 | convolution fusion | flops 1621098496 | bytes 6963200 | tf_op jit(solution)/shard_map/cghqk,ckghp->cqghp/dot_general | solution.py:82
  126.5 2.2 all-gather.12.cloned.1.call-done
  128.7 12.8 %fusion.2 = f32[16,1,64,128]{3,1,2,0:T(1,128)S(1)} fusion(f32[16,16,1,1]{0,2,3,1:T(1,128)S(1)} %copy.95, f32[16,16,64,128]{3,2,1,0:T(8,128)} %all-gather.12.cloned.1.call-done), kind=kOutput, calls=%fused_computation.9 | convolution fusion | flops 25165824 | bytes 8913920 | tf_op jit(solution)/shard_map/jgh,jghpn->ghpn/dot_general | solution.py:110
  141.6 5.2 %fusion.19 = f32[8,128,1,16,64]{1,4,3,0,2:T(8,128)S(1)} fusion(f32[8,16,64,128]{3,2,1,0:T(8,128)S(1)} %copy-done.6, f32[8,16,64,128]{3,2,1,0:T(8,128)} %fusion.4, f32[8,128,1,16,64]{1,0,4,3,2:T(8,128)S(1)} %bitcast.169, f32[16,64,128,1]{2,1,0,3:T(8,128)S(1)} %bitcast.180, bf16[8,128,128,1]{2,1,3,0:T(8,128)(2,1)S(1)} %bitcast.176, f32[16]{0:T(128)S(1)} %copy-done.13, ...), kind=kOutput, calls=%fused_computation.35 | convolution fusion | flops 1616904192 | bytes 17694784 | tf_op jit(solution)/shard_map/cqgn,ghpn->cqghp/dot_general | solution.py:113
  146.8 3.3 copy.90
  150.1 4.0 %multiply_reduce_fusion.1 = (f32[1024]{0:T(1024)S(1)}, f32[1024,1024]{0,1:T(8,128)}) fusion(bf16[1024,1024]{0,1:T(8,128)(2,1)S(1)} %copy-done.7, f32[128,8,8,128]{3,2,1,0:T(8,128)S(1)} %bitcast.170), kind=kLoop, calls=%fused_computation.45 | loop fusion | flops 8387584 | bytes 10489856 | tf_op jit(solution)/shard_map/reduce_sum | solution.py:121
  154.2 66.4 %all-gather.8.cloned.1.call-done = bf16[96,1024,64]{1,2,0:T(8,128)(2,1)} async-done(((bf16[6,1024,64]{1,2,0:T(8,128)(2,1)}), bf16[96,1024,64]{1,2,0:T(8,128)(2,1)}) %all-gather.8.cloned.1.call-update) | async-done | bytes 12582928 | tf_op jit(solution)/shard_map/all_gather | solution.py:132
  220.5 5.1 %gather_fusion.2 = bf16[3,1024,64]{1,2,0:T(8,128)(2,1)S(1)} fusion(bf16[96,1024,64]{1,2,0:T(8,128)(2,1)} %all-gather.8.cloned.1.call-done, s32[1024]{0:T(1024)S(1)} %pad_clamp_fusion), kind=kCustom, calls=%fused_computation.2 | custom fusion | bytes 786444 | tf_op jit(solution)/shard_map/jit(_take)/gather | solution.py:135
  225.8 2.9 fusion.59
  229.5 15.6 %convolution_convert_fusion = bf16[1024,4096]{1,0:T(8,128)(2,1)} fusion(bf16[1024,4096]{1,0:T(8,128)(2,1)} %param.30, f32[1024,1024]{0,1:T(8,128)} %get-tuple-element.84, f32[1024]{0:T(1024)S(1)} %convert_element_type.84, f32[1024]{0:T(1024)S(1)} %add_rsqrt_fusion), kind=kOutput, calls=%fused_computation.18 | convolution fusion | flops 8597274624 | bytes 20979712 | tf_op jit(solution)/shard_map/dot_general | solution.py:138
  245.1 38.6 %all-gather.10.cloned.1.call-done = bf16[96,64,512]{2,1,0:T(8,128)(2,1)} async-done(((bf16[6,64,512]{2,1,0:T(8,128)(2,1)}), bf16[96,64,512]{2,1,0:T(8,128)(2,1)}) %all-gather.10.cloned.1.call-update) | async-done | bytes 6291472 | tf_op jit(solution)/shard_map/all_gather | solution.py:133
  283.8 3.3 gather_fusion.3
  287.1 23.0 %all-gather.14.cloned.1.call-done = f32[8192,64]{0,1:T(8,128)} async-done(((f32[1024,64]{0,1:T(8,128)}), f32[8192,64]{0,1:T(8,128)}) %all-gather.14.cloned.1.call-update) | async-done | bytes 2097168 | tf_op jit(solution)/shard_map/all_gather | solution.py:149
  310.1 2.8 copy.105
  314.6 50.5 %reduce-scatter.2.cloned.1.call-done = bf16[1024,512]{1,0:T(8,128)(2,1)} async-done(((bf16[1024,4096]{1,0:T(8,128)(2,1)}), bf16[1024,512]{1,0:T(8,128)(2,1)}) %reduce-scatter.2.cloned.1.call-update) | async-done | bytes 1048592 | tf_op jit(solution)/shard_map/reduce_scatter | solution.py:137
  365.1 2.6 add_convert_fusion
  (125 shorter events, 30.3 us)
Async XLA Ops:
  6.5 93.7 %copy-start = (s32[32]{0:T(128)S(1)}, s32[32]{0:T(128)}, u32[]{:S(2)}) copy-start(s32[32]{0:T(128)} %param.34) | copy-start | bytes 388
  6.5 21.5 %copy-start.9 = (bf16[1024,128]{1,0:T(8,128)(2,1)S(1)}, bf16[1024,128]{1,0:T(8,128)(2,1)}, u32[]{:S(2)}) copy-start(bf16[1024,128]{1,0:T(8,128)(2,1)} %param.20) | copy-start | bytes 786436
  6.5 122.1 %all-gather.12.cloned.1.call-start = ((), (), s32[]{:S(2)}) async-start(), calls=%async_computation.4 | async-start | bytes 8912896 | tf_op jit(solution)/shard_map/all_gather | solution.py:102
  8.2 20.3 %collective-permute-start = (bf16[3,1024]{0,1:T(8,128)(2,1)}, bf16[3,1024]{0,1:T(8,128)(2,1)S(1)}, u32[]{:S(2)}, u32[]{:S(2)}) collective-permute-start(bf16[3,1024]{0,1:T(8,128)(2,1)} %copy.73), channel_id=1, source_target_pairs={{0,8},{8,16},{16,24},{24,32},{32,40},{40,48},{48,56},{56,64},{64,7... | collective-permute-start | bytes 18440 | tf_op jit(solution)/shard_map/ppermute | solution.py:19
  12.8 15.2 %collective-permute-start.2 = (bf16[3,128]{1,0:T(4,128)(2,1)S(1)}, bf16[3,128]{1,0:T(4,128)(2,1)S(1)}, u32[]{:S(2)}, u32[]{:S(2)}) collective-permute-start(bf16[3,128]{1,0:T(4,128)(2,1)S(1)} %slice.104), channel_id=1, source_target_pairs={{0,8},{8,16},{16,24},{24,32},{32,40},{40,48},{48,56},{56,64},{64,7... | collective-permute-start | bytes 2312 | tf_op jit(solution)/shard_map/ppermute | solution.py:19
  40.0 18.7 %copy-start.10 = (bf16[1024,128]{1,0:T(8,128)(2,1)S(1)}, bf16[1024,128]{1,0:T(8,128)(2,1)}, u32[]{:S(2)}) copy-start(bf16[1024,128]{1,0:T(8,128)(2,1)} %param.21) | copy-start | bytes 786436
  40.0 22.3 %copy-start.15 = (u32[128]{0:T(128)S(1)}, u32[128]{0:T(128)}, u32[]{:S(2)}) copy-start(u32[128]{0:T(128)} %constant.114) | copy-start | bytes 1540
  40.0 60.9 %copy-start.2 = (s32[96]{0:T(128)S(1)}, s32[96]{0:T(128)}, u32[]{:S(2)}) copy-start(s32[96]{0:T(128)} %param.35) | copy-start | bytes 1156
  40.0 61.6 %copy-start.14 = (s32[32]{0:T(128)S(1)}, s32[32]{0:T(128)}, u32[]{:S(2)}) copy-start(s32[32]{0:T(128)} %param.33) | copy-start | bytes 388
  40.0 61.9 %copy-start.11 = (bf16[4,128]{1,0:T(4,128)(2,1)S(1)}, bf16[4,128]{1,0:T(4,128)(2,1)}, u32[]{:S(2)}) copy-start(bf16[4,128]{1,0:T(4,128)(2,1)} %param.28) | copy-start | bytes 3076
  56.4 0.8 copy-start.3
  56.4 49.9 %copy-start.12 = (bf16[1024]{0:T(1024)(128)(2,1)S(1)}, bf16[1024]{0:T(1024)(128)(2,1)}, u32[]{:S(2)}) copy-start(bf16[1024]{0:T(1024)(128)(2,1)} %param.29) | copy-start | bytes 6148
  57.2 163.3 %all-gather.8.cloned.1.call-start = ((), (), s32[]{:S(2)}) async-start(), calls=%async_computation.2 | async-start | bytes 13369344 | tf_op jit(solution)/shard_map/all_gather | solution.py:132
  57.9 225.8 %all-gather.10.cloned.1.call-start = ((), (), s32[]{:S(2)}) async-start(), calls=%async_computation.3 | async-start | bytes 6684672 | tf_op jit(solution)/shard_map/all_gather | solution.py:133
  58.7 251.4 %all-gather.14.cloned.1.call-start = ((), (), s32[]{:S(2)}) async-start(), calls=%async_computation.5 | async-start | bytes 2359296 | tf_op jit(solution)/shard_map/all_gather | solution.py:149
  58.8 47.5 %collective-permute-start.1 = (bf16[3,128]{1,0:T(4,128)(2,1)S(1)}, bf16[3,128]{1,0:T(4,128)(2,1)S(1)}, u32[]{:S(2)}, u32[]{:S(2)}) collective-permute-start(bf16[3,128]{1,0:T(4,128)(2,1)S(1)} %slice.95), channel_id=1, source_target_pairs={{0,8},{8,16},{16,24},{24,32},{32,40},{40,48},{48,56},{56,64},{64,7... | collective-permute-start | bytes 2312 | tf_op jit(solution)/shard_map/ppermute | solution.py:19
  106.3 2.4 copy-start.4
  108.6 3.1 copy-start.8
  126.5 15.1 %copy-start.13 = (f32[16]{0:T(128)S(1)}, f32[16]{0:T(128)}, u32[]{:S(2)}) copy-start(f32[16]{0:T(128)} %param.25) | copy-start | bytes 196
  128.7 12.9 %copy-start.5 = (f32[128,8,8,128]{3,2,1,0:T(8,128)S(1)}, f32[128,8,8,128]{3,2,1,0:T(8,128)}, u32[]{:S(2)}) copy-start(f32[128,8,8,128]{3,2,1,0:T(8,128)} %copy.103) | copy-start | bytes 12582916
  128.7 12.9 %copy-start.6 = (f32[8,16,64,128]{3,2,1,0:T(8,128)S(1)}, f32[8,16,64,128]{3,2,1,0:T(8,128)}, u32[]{:S(2)}) copy-start(f32[8,16,64,128]{3,2,1,0:T(8,128)} %fusion.21) | copy-start | bytes 12582916
  146.8 3.3 copy-start.7
  229.5 135.6 %reduce-scatter.2.cloned.1.call-start = ((), (), s32[]{:S(2)}) async-start(), calls=%async_computation.1 | async-start | bytes 9437184 | tf_op jit(solution)/shard_map/reduce_scatter | solution.py:137
  313.0 54.8 %copy-start.1 = (s32[32]{0:T(128)S(1)}, s32[32]{0:T(128)}, u32[]{:S(2)}) copy-start(s32[32]{0:T(128)} %param.34) | copy-start | bytes 388
Sparse Core Ops, SparseCore 0:
  57.3 71.3 all-gather.11
  130.9 89.6 all-gather.7
  222.7 60.9 all-gather.9
  285.3 24.7 all-gather.13
  312.3 52.7 reduce-scatter.1
